TPU v7x, 512 devices: a 8x2x16 block of a 8x16x16 slice. The times are simulated.
512 devices in a mesh: rep: 2 (over y), blk: 128 (over z, x), head: 2 (over core).
Axes of the slice: x: 8, y: 2, z: 16, core: 2. Of those that a mesh axis runs over, the one named last changes fastest.
The devices are a block of a 8x16x16 slice.
Arguments:
- queries: bfloat16 [2, 8192, 8192], P('rep', 'blk', 'head'), parts along dimension 0, may hold values from -200 to 200
- keys: bfloat16 [2, 8192, 512], P('rep', 'blk', 'head'), parts along dimension 0, may hold values from -6 to 6
- values: bfloat16 [2, 8192, 512], P('rep', 'blk', 'head'), parts along dimension 0, may hold values from -6 to 6
- prompt_length: int32 [2], P('rep'), parts along dimension 0, may hold values from 4096 to 8192
- span_order: int32 [512], P('rep'), parts along dimension 0, may hold values from 0 to 255, as said below
Outputs:
- attended: bfloat16 [2, 8192, 8192], P('rep', 'blk', 'head'), parts along dimension 0
There are 2 independent parts, one for each index of `rep`. A program takes and returns all parts, laid end to end along the dimension named above; each array names one. Nothing has to cross between parts.
Inputs may be any that keep to these rules, and one draw needn't show every extreme that they name: `span_order`: each of the 256 span numbers stands in exactly one slot.
All inputs are finite; a program needn't handle non-finite values.
Results may differ from a plain program's by a relative error of at most 0.0065.
Values may be sent and summed in bfloat16 or wider, within the bound.
No kernel may reach another device: no remote copies, remote signals or barrier semaphores. Data moves between devices by JAX's collectives and lax.ppermute only.
A program may use at most 64 MiB of HBM per device.

v0:
```python
import jax
import jax.numpy as jnp
from jax import lax
from jax.sharding import Mesh
from jax.sharding import PartitionSpec as P

HEAD_WIDTH = 128
BLK = ("blk_0", "blk_1")
NEG_FILL = -1e30


def laid_out(pieces, dim):
    pieces = jnp.moveaxis(pieces, 0, dim)
    shape = pieces.shape
    return pieces.reshape(*shape[:dim], shape[dim] * shape[dim + 1], *shape[dim + 2 :])


def stacked_from(value, axes, sequence):
    pieces = value[None]
    for k in sequence:
        pieces = lax.all_gather(pieces, axes[k], axis=0, tiled=True)
    carried = [lax.axis_size(axes[k]) for k in reversed(sequence)]
    pieces = pieces.reshape(*carried, *value.shape)
    turned = sorted(range(len(sequence)), key=lambda place: sequence[len(sequence) - 1 - place])
    return pieces.transpose(*turned, *range(len(sequence), pieces.ndim)).reshape(-1, *value.shape)


def whole_of(value, axes, sequence, dim):
    return laid_out(stacked_from(value, axes, sequence), dim)


def shards(queries, keys, values, prompt_length, span_order):
    mine = lax.axis_index(BLK)
    prompts = queries.shape[0]
    tok_rows = queries.shape[1]
    span = tok_rows // 2
    local_heads = keys.shape[2] // HEAD_WIDTH
    group = queries.shape[2] // (local_heads * HEAD_WIDTH)
    offsets = jnp.arange(span, dtype=jnp.int32)
    all_pos = (span_order[:, None] * span + offsets[None, :]).reshape(-1)
    my_pos = lax.dynamic_slice_in_dim(all_pos, mine * tok_rows, tok_rows)
    row_pos = jnp.tile(my_pos, group)
    q_cols = (
        queries.reshape(prompts, tok_rows, local_heads, group, HEAD_WIDTH)
        .transpose(0, 2, 4, 3, 1)
        .reshape(prompts, local_heads, HEAD_WIDTH, group * tok_rows)
    )
    scale = HEAD_WIDTH ** (-0.5)

    def attend(carry, key_rows, value_rows, key_pos):
        best, total, accum = carry
        count = key_rows.shape[1]
        key_four = key_rows.reshape(prompts, count, local_heads, HEAD_WIDTH)
        value_four = value_rows.reshape(prompts, count, local_heads, HEAD_WIDTH)
        scores = (
            jnp.einsum("skhd,shdr->shkr", key_four, q_cols, preferred_element_type=jnp.float32)
            * scale
        )
        allowed = (key_pos[None, :, None] <= row_pos[None, None, :]) & (
            key_pos[None, :, None] < prompt_length[:, None, None]
        )
        scores = jnp.where(allowed[:, None], scores, NEG_FILL)
        fresh = jnp.maximum(best, jnp.max(scores, axis=2))
        weights = jnp.where(allowed[:, None], jnp.exp(scores - fresh[:, :, None, :]), 0.0)
        factor = jnp.exp(best - fresh)
        total = total * factor + jnp.sum(weights, axis=2)
        mixed = jnp.einsum(
            "shkr,skhd->shrd",
            weights.astype(jnp.bfloat16),
            value_four,
            preferred_element_type=jnp.float32,
        )
        accum = accum * factor[..., None] + mixed
        return (fresh, total, accum)

    def visit(carry, key_rows, value_rows, key_pos):
        return attend(carry, key_rows, value_rows, key_pos)

    def fold_piece(carry, pieces):
        key_rows, value_rows = pieces
        rows = key_rows.shape[1]
        size = max((d for d in range(1, min(rows, 256) + 1) if rows % d == 0))
        steps = rows // size
        if steps == 1:
            return visit(carry, key_rows, value_rows, all_pos)

        def one_block(index, state):
            begin = (index * size).astype(jnp.int32)
            return visit(
                state,
                lax.dynamic_slice_in_dim(key_rows, begin, size, 1),
                lax.dynamic_slice_in_dim(value_rows, begin, size, 1),
                lax.dynamic_slice_in_dim(all_pos, begin, size),
            )

        return lax.fori_loop(0, steps, one_block, carry)

    width = group * tok_rows
    init = (
        jnp.full((prompts, local_heads, width), NEG_FILL, jnp.float32),
        jnp.zeros((prompts, local_heads, width), jnp.float32),
        jnp.zeros((prompts, local_heads, width, HEAD_WIDTH), jnp.float32),
    )
    carry = fold_piece(init, (whole_of(keys, BLK, (0, 1), 1), whole_of(values, BLK, (0, 1), 1)))
    best, total, accum = carry
    normed = accum / total[..., None]
    joined_heads = (
        normed.reshape(prompts, local_heads, group, tok_rows, HEAD_WIDTH)
        .transpose(0, 3, 1, 2, 4)
        .reshape(prompts, tok_rows, local_heads * group * HEAD_WIDTH)
    )
    joined_heads = jnp.where(
        (my_pos[None, :] < prompt_length[:, None])[:, :, None], joined_heads, 0.0
    )
    return joined_heads.astype(jnp.bfloat16)


def solution(mesh):
    split = Mesh(
        mesh.devices.reshape(mesh.shape["rep"], 16, 8, mesh.shape["head"]),
        ("rep", "blk_0", "blk_1", "head"),
    )
    in_specs = (
        P("rep", BLK, "head"),
        P("rep", BLK, "head"),
        P("rep", BLK, "head"),
        P("rep"),
        P("rep"),
    )
    out_specs = P("rep", BLK, "head")
    return jax.shard_map(
        shards, mesh=split, in_specs=in_specs, out_specs=out_specs, check_vma=False
    )
```

profile of v0, /device:TPU:65, one launch (start us, length us, event | category | flops | bytes accessed | tf_op | source)
XLA Modules:
  0.0 430.8 jit_solution(16120057133728882408)
XLA Ops:
  6.6 67.5 %all-gather = bf16[16,64,256]{2,1,0:T(8,128)(2,1)} all-gather(bf16[1,64,256]{2,1,0:T(8,128)(2,1)} %param.8), channel_id=2, replica_groups=mesh['rep'=2,'blk_0'=16,'blk_1'=8,'head'=2] {'blk_0'}, dimensions={0}, use_global_device_ids=true | all-gather | bytes 557056 | tf_op jit(solution)/shard_map/all_gather | solution.py:21
  74.2 25.9 %all-gather.2 = bf16[16,64,256]{2,1,0:T(8,128)(2,1)} all-gather(bf16[1,64,256]{2,1,0:T(8,128)(2,1)} %param.9), channel_id=4, replica_groups=mesh['rep'=2,'blk_0'=16,'blk_1'=8,'head'=2] {'blk_0'}, dimensions={0}, use_global_device_ids=true | all-gather | bytes 557056 | tf_op jit(solution)/shard_map/all_gather | solution.py:21
  101.6 33.6 %all-gather.7.cloned.1.call-done = bf16[128,64,256]{2,1,0:T(8,128)(2,1)} async-done(((bf16[16,64,256]{2,1,0:T(8,128)(2,1)}), bf16[128,64,256]{2,1,0:T(8,128)(2,1)}) %all-gather.7.cloned.1.call-update) | async-done | bytes 4194320 | tf_op jit(solution)/shard_map/all_gather | solution.py:21
  135.2 4.7 %copy.39 = bf16[16,8,1,64,256]{4,3,1,0,2:T(8,128)(2,1)} copy(bf16[16,8,1,64,256]{4,3,0,1,2:T(8,128)(2,1)} %bitcast.69) | data formatting | bytes 8388608 | tf_op jit(solution)/shard_map/transpose | solution.py:25
  139.9 57.4 %all-gather.9.cloned.1.call-done = bf16[128,64,256]{2,1,0:T(8,128)(2,1)} async-done(((bf16[16,64,256]{2,1,0:T(8,128)(2,1)}), bf16[128,64,256]{2,1,0:T(8,128)(2,1)}) %all-gather.9.cloned.1.call-update) | async-done | bytes 4194320 | tf_op jit(solution)/shard_map/all_gather | solution.py:21
  197.4 4.8 %copy.41 = bf16[16,8,1,64,256]{4,3,1,0,2:T(8,128)(2,1)} copy(bf16[16,8,1,64,256]{4,3,0,1,2:T(8,128)(2,1)} %bitcast.70) | data formatting | bytes 8388608 | tf_op jit(solution)/shard_map/transpose | solution.py:25
  202.1 218.6 %while.18 = (s32[]{:T(128)}, f32[1,2,1024]{2,1,0:T(2,128)S(1)}, f32[1,2,1024]{2,1,0:T(2,128)S(1)}, f32[1,2,1024,128]{3,2,1,0:T(8,128)}, s32[8192]{0:T(1024)S(1)}...) while((s32[]{:T(128)}, f32[1,2,1024]{2,1,0:T(2,128)S(1)}, ...), condition=%wide.region_3.4_spmd.clone, body=%wide.region_0.3_spmd.clone.sunk | while | flops 276574464 | bytes 11423691 | solution.py:96
  203.2 1.0 constant_dynamic-slice_fusion.3
  205.1 2.1 fusion.33
  208.8 1.0 constant_dynamic-slice_fusion.3
  210.7 3.3 fusion.33
  215.7 1.0 constant_dynamic-slice_fusion.3
  217.6 3.3 fusion.33
  222.6 1.0 constant_dynamic-slice_fusion.3
  224.5 3.3 fusion.33
  229.5 1.0 constant_dynamic-slice_fusion.3
  231.4 3.3 fusion.33
  236.3 1.0 constant_dynamic-slice_fusion.3
  238.2 3.3 fusion.33
  243.2 1.0 constant_dynamic-slice_fusion.3
  245.1 3.3 fusion.33
  250.1 1.0 constant_dynamic-slice_fusion.3
  252.0 3.3 fusion.33
  256.9 1.0 constant_dynamic-slice_fusion.3
  258.8 3.3 fusion.33
  263.8 1.0 constant_dynamic-slice_fusion.3
  265.7 3.3 fusion.33
  270.7 1.0 constant_dynamic-slice_fusion.3
  272.6 3.3 fusion.33
  277.6 1.0 constant_dynamic-slice_fusion.3
  279.5 3.3 fusion.33
  284.4 1.0 constant_dynamic-slice_fusion.3
  286.3 3.3 fusion.33
  291.3 1.0 constant_dynamic-slice_fusion.3
  293.2 3.3 fusion.33
  298.2 1.0 constant_dynamic-slice_fusion.3
  300.1 3.3 fusion.33
  305.0 1.0 constant_dynamic-slice_fusion.3
  306.9 3.3 fusion.33
  313.8 3.3 fusion.33
  320.7 3.3 fusion.33
  325.7 1.0 constant_dynamic-slice_fusion.3
  327.6 3.3 fusion.33
  332.5 1.0 constant_dynamic-slice_fusion.3
  334.4 3.3 fusion.33
  339.4 1.0 constant_dynamic-slice_fusion.3
  341.3 3.3 fusion.33
  346.3 1.0 constant_dynamic-slice_fusion.3
  348.2 3.3 fusion.33
  353.1 1.0 constant_dynamic-slice_fusion.3
  355.0 3.3 fusion.33
  360.0 1.0 constant_dynamic-slice_fusion.3
  361.9 3.3 fusion.33
  366.9 1.0 constant_dynamic-slice_fusion.3
  368.8 3.3 fusion.33
  373.8 1.0 constant_dynamic-slice_fusion.3
  375.7 3.3 fusion.33
  382.5 3.3 fusion.33
  389.4 3.3 fusion.33
  396.3 3.3 fusion.33
  403.1 3.3 fusion.33
  410.0 3.3 fusion.33
  416.9 3.3 fusion.33
  420.8 1.6 broadcast_divide_fusion
  (381 shorter events, 90.7 us)
Async XLA Ops:
  6.5 93.6 %copy-start.1 = (s32[256]{0:T(256)S(1)}, s32[256]{0:T(256)}, u32[]{:S(2)}) copy-start(s32[256]{0:T(256)} %param.11) | copy-start | bytes 3076
  6.5 94.5 %copy-start = (bf16[1,64,4096]{2,1,0:T(8,128)(2,1)S(1)}, bf16[1,64,4096]{2,1,0:T(8,128)(2,1)}, u32[]{:S(2)}) copy-start(bf16[1,64,4096]{2,1,0:T(8,128)(2,1)} %param.7) | copy-start | bytes 1572868
  6.6 128.7 %all-gather.7.cloned.1.call-start = ((), (), s32[]{:S(2)}) async-start(), calls=%async_computation | async-start | bytes 4718592 | tf_op jit(solution)/shard_map/all_gather | solution.py:21
  74.1 123.3 %all-gather.9.cloned.1.call-start = ((), (), s32[]{:S(2)}) async-start(), calls=%async_computation.1 | async-start | bytes 4718592 | tf_op jit(solution)/shard_map/all_gather | solution.py:21
Sparse Core Ops, SparseCore 0:
  74.2 60.9 all-gather.6
  137.3 60.0 all-gather.8
where the time goes:
time: 433 us; the launch traced here: 431 us
  matrix products  125 us (29%)
  blocking collectives  93.4 us (22%)
  waiting for transfers between devices  91.1 us (21%)
  other arithmetic  53.3 us (12%)
  local copies, waits for them, and re-layouts  51.2 us (12%)
  between operations  14.2 us (3%)
    dot_general x32, matrix products, attend(): jnp.einsum('shkr,skhd->shrd', weights.astype(jnp.bfloat16), value_four, p...  104 us
    all_gather x2, blocking collectives, stacked_from(): pieces = lax.all_gather(pieces, axes[k], axis=0, tiled=True)  93.4 us
    all_gather x2, waiting for transfers between devices, stacked_from(): pieces = lax.all_gather(pieces, axes[k], axis=0, tiled=True)  91 us
    dynamic_slice x64, local copies, waits for them, and re-layouts, one_block(): lax.dynamic_slice_in_dim(value_rows, begin, size, 1)  34.9 us
    lt x32, other arithmetic, attend(): key_pos[None, :, None] < prompt_length[:, None, None]  23.3 us
    dot_general x32, matrix products, attend(): jnp.einsum('skhd,shdr->shkr', key_four, q_cols, preferred_element_type=jn...  20.9 us
    reduce_sum x32, other arithmetic, attend(): total = total * factor + jnp.sum(weights, axis=2)  18.2 us
    transpose x2, local copies, waits for them, and re-layouts, stacked_from(): pieces.transpose(*turned, *range(len(sequence), pieces.ndim))  9.46 us
  transfers between devices with their start and end apart: 2, of which 2 were waited for; matrix products, arithmetic and copies ran while one was open for 1% of the time, Pallas kernels for 0%

commit v1 on v0

--- a/solution.py
+++ b/solution.py
@@ -9,6 +9,11 @@
 NEG_FILL = -1e30
 
 
+def all_by_exchange(x, axis, d):
+    sent = jnp.stack([x] * lax.axis_size(axis))
+    return jnp.concatenate(lax.all_to_all(sent, axis, 0, 0), axis=d)
+
+
 def laid_out(pieces, dim):
     pieces = jnp.moveaxis(pieces, 0, dim)
     shape = pieces.shape
@@ -18,7 +23,7 @@
 def stacked_from(value, axes, sequence):
     pieces = value[None]
     for k in sequence:
-        pieces = lax.all_gather(pieces, axes[k], axis=0, tiled=True)
+        pieces = all_by_exchange(pieces, axes[k], 0)
     carried = [lax.axis_size(axes[k]) for k in reversed(sequence)]
     pieces = pieces.reshape(*carried, *value.shape)
     turned = sorted(range(len(sequence)), key=lambda place: sequence[len(sequence) - 1 - place])

time: 433 us -> 531 us (1.23)
  the two profiles are of different devices: /device:TPU:65 before, /device:TPU:320 now
where the time goes in v1:
time: 531 us; the launch traced here: 529 us
  blocking collectives  204 us (38%)
  matrix products  123 us (23%)
  waiting for transfers between devices  84.4 us (16%)
  local copies, waits for them, and re-layouts  55.8 us (11%)
  other arithmetic  53.3 us (10%)
    all_to_all x3, blocking collectives, all_by_exchange(): return jnp.concatenate(lax.all_to_all(sent, axis, 0, 0), axis=d)  204 us
    dot_general x32, matrix products, attend(): jnp.einsum('shkr,skhd->shrd', weights.astype(jnp.bfloat16), value_four, p...  102 us
    all_to_all x1, waiting for transfers between devices, all_by_exchange(): return jnp.concatenate(lax.all_to_all(sent, axis, 0, 0), axis=d)  84.4 us
    dynamic_slice x64, local copies, waits for them, and re-layouts, one_block(): lax.dynamic_slice_in_dim(value_rows, begin, size, 1)  34.9 us
    lt x32, other arithmetic, attend(): key_pos[None, :, None] < prompt_length[:, None, None]  23.3 us
    dot_general x32, matrix products, attend(): jnp.einsum('skhd,shdr->shkr', key_four, q_cols, preferred_element_type=jn...  20.7 us
    reduce_sum x32, other arithmetic, attend(): total = total * factor + jnp.sum(weights, axis=2)  18.2 us
  transfers between devices with their start and end apart: 1, of which 1 were waited for; matrix products, arithmetic and copies ran while one was open for 1% of the time, Pallas kernels for 0%

profile of v1, /device:TPU:320, one launch (start us, length us, event | category | flops | bytes accessed | tf_op | source)
XLA Modules:
  0.0 528.8 jit_solution(12692148792876400360)
XLA Ops:
  0.8 69.7 %all_to_all.20 = bf16[16,1,1,64,256]{4,3,2,1,0:T(8,128)(2,1)S(1)} all-to-all(bf16[16,1,1,64,256]{4,3,2,1,0:T(8,128)(2,1)S(1)} %stack.14), channel_id=1, replica_groups=mesh['rep'=2,'blk_0'=16,'blk_1'=8,'head'=2] {'blk_0'}, dimensions={0} | all-to-all | bytes 1048576 | tf_op jit(solution)/shard_map/all_to_all | solution.py:14
  71.3 35.3 %all_to_all.21 = bf16[16,1,1,64,256]{4,3,2,1,0:T(8,128)(2,1)S(1)} all-to-all(bf16[16,1,1,64,256]{4,3,2,1,0:T(8,128)(2,1)S(1)} %stack.12), channel_id=1, replica_groups=mesh['rep'=2,'blk_0'=16,'blk_1'=8,'head'=2] {'blk_0'}, dimensions={0} | all-to-all | bytes 1048576 | tf_op jit(solution)/shard_map/all_to_all | solution.py:14
  107.2 99.2 %all_to_all.22 = bf16[8,16,1,64,256]{4,3,1,2,0:T(8,128)(2,1)} all-to-all(bf16[8,16,1,64,256]{4,3,1,2,0:T(8,128)(2,1)S(1)} %stack.15), channel_id=1, replica_groups=mesh['rep'=2,'blk_0'=16,'blk_1'=8,'head'=2] {'blk_1'}, dimensions={0} | all-to-all | bytes 8388608 | tf_op jit(solution)/shard_map/all_to_all | solution.py:14
  206.4 2.5 stack.13
  208.9 4.9 all-to-all-start.1
  215.3 4.7 copy.29
  220.0 84.4 %all-to-all-done.1 = bf16[8,16,1,64,256]{4,3,1,2,0:T(8,128)(2,1)} async-done(((bf16[8,16,1,64,256]{4,3,1,2,0:T(8,128)(2,1)}), bf16[8,16,1,64,256]{4,3,1,2,0:T(8,128)(2,1)}, u32[]{:S(2)}, u32[]{:S(2)}) %all-to-all-start.1) | async-done | bytes 4194336 | tf_op jit(solution)/shard_map/all_to_all | solution.py:14
  304.5 4.7 copy.27
  309.2 216.5 %while.18 = (s32[]{:T(128)}, f32[1,2,1024]{2,1,0:T(2,128)S(1)}, f32[1,2,1024]{2,1,0:T(2,128)S(1)}, f32[1,2,1024,128]{3,2,1,0:T(8,128)}, s32[8192]{0:T(1024)S(1)}...) while((s32[]{:T(128)}, f32[1,2,1024]{2,1,0:T(2,128)S(1)}, ...), condition=%wide.region_3.4_spmd.clone, body=%wide.region_0.3_spmd.clone.sunk | while | flops 276574464 | bytes 11423691 | solution.py:101
  310.2 1.0 constant_dynamic-slice_fusion.3
  312.1 2.0 fusion.33
  317.7 3.2 fusion.33
  322.6 1.0 constant_dynamic-slice_fusion.3
  324.5 3.2 fusion.33
  331.3 3.2 fusion.33
  336.2 1.0 constant_dynamic-slice_fusion.3
  338.1 3.2 fusion.33
  343.0 1.0 constant_dynamic-slice_fusion.3
  344.9 3.2 fusion.33
  349.9 1.0 constant_dynamic-slice_fusion.3
  351.7 3.2 fusion.33
  356.7 1.0 constant_dynamic-slice_fusion.3
  358.5 3.2 fusion.33
  363.5 1.0 constant_dynamic-slice_fusion.3
  365.4 3.2 fusion.33
  370.3 1.0 constant_dynamic-slice_fusion.3
  372.2 3.2 fusion.33
  377.1 1.0 constant_dynamic-slice_fusion.3
  379.0 3.2 fusion.33
  383.9 1.0 constant_dynamic-slice_fusion.3
  385.8 3.2 fusion.33
  390.7 1.0 constant_dynamic-slice_fusion.3
  392.6 3.2 fusion.33
  397.5 1.0 constant_dynamic-slice_fusion.3
  399.4 3.2 fusion.33
  404.3 1.0 constant_dynamic-slice_fusion.3
  406.2 3.2 fusion.33
  411.1 1.0 constant_dynamic-slice_fusion.3
  413.0 3.2 fusion.33
  417.9 1.0 constant_dynamic-slice_fusion.3
  419.8 3.2 fusion.33
  424.7 1.0 constant_dynamic-slice_fusion.3
  426.6 3.2 fusion.33
  431.5 1.0 constant_dynamic-slice_fusion.3
  433.4 3.2 fusion.33
  438.3 1.0 constant_dynamic-slice_fusion.3
  440.2 3.2 fusion.33
  447.0 3.2 fusion.33
  451.9 1.0 constant_dynamic-slice_fusion.3
  453.8 3.2 fusion.33
  460.6 3.2 fusion.33
  465.5 1.0 constant_dynamic-slice_fusion.3
  467.4 3.2 fusion.33
  472.3 1.0 constant_dynamic-slice_fusion.3
  474.2 3.2 fusion.33
  479.1 1.0 constant_dynamic-slice_fusion.3
  481.0 3.2 fusion.33
  487.8 3.2 fusion.33
  494.6 3.2 fusion.33
  501.4 3.2 fusion.33
  508.2 3.2 fusion.33
  515.0 3.2 fusion.33
  521.8 3.2 fusion.33
  525.7 1.6 broadcast_divide_fusion
  (382 shorter events, 94.5 us)
Async XLA Ops:
  208.9 5.0 copy-start.1
  208.9 5.8 %copy-start = (bf16[1,64,4096]{2,1,0:T(8,128)(2,1)S(1)}, bf16[1,64,4096]{2,1,0:T(8,128)(2,1)}, u32[]{:S(2)}) copy-start(bf16[1,64,4096]{2,1,0:T(8,128)(2,1)} %param.7) | copy-start | bytes 1572868
  208.9 95.6 %all-to-all-start.1 = ((bf16[8,16,1,64,256]{4,3,1,2,0:T(8,128)(2,1)}), bf16[8,16,1,64,256]{4,3,1,2,0:T(8,128)(2,1)}, u32[]{:S(2)}, u32[]{:S(2)}) async-start(bf16[8,16,1,64,256]{4,3,1,2,0:T(8,128)(2,1)} %stack.13), calls=%async_computation.1 | async-start | bytes 8388608 | tf_op jit(solution)/shard_map/all_to_all | solution.py:14
